TPU v7x, 512 devices: a whole 4x8x8 slice. The times are simulated.
512 devices in a mesh: prow: 16 (over z, core), pcol: 32 (over y, x).
Axes of the slice: x: 4, y: 8, z: 8, core: 2. Of those that a mesh axis runs over, the one named last changes fastest.
Arguments:
- tiles: bfloat16 [16, 32, 32, 256, 256], P('prow', 'pcol')
- tile_brow: int32 [16, 32, 32], P('prow', 'pcol'), may hold values from 0 to 31, as said below
- tile_bcol: int32 [16, 32, 32], P('prow', 'pcol'), may hold values from 0 to 15, as said below
- tile_count: int32 [16, 32], P('prow', 'pcol'), may hold values from 8 to 32, as said below
Outputs:
- row_scale: float32 [32, 16, 256], P(None, 'prow')
- col_scale: float32 [16, 32, 256], P(None, 'pcol')
Inputs may be any that keep to these rules, and one draw needn't show every extreme that they name: `tile_brow`: on one device, no two slots name the same pair of local block row and column; the diagonal tile of every block row is present and live, in the first slots of the device that holds it. `tile_bcol`: see tile_brow. `tile_count`: a device that holds diagonal tiles has all 32 slots live, every other device at most 16.
All inputs are finite; a program needn't handle non-finite values.
Results may differ from a plain program's by a relative error of at most 0.0003.
Values sent between devices are 32-bit elements; how exact they have to be, the bound alone decides.
A program may use at most 64 MiB of HBM per device.

v0:
```python
import jax
import jax.numpy as jnp
from jax import lax
from jax.sharding import Mesh
from jax.sharding import PartitionSpec as P

BR_DEV = 32
SWEEPS = 3
PCOL = ("pcol_0", "pcol_1")


def one_axis_at_a_time(value, axes):
    for axis in axes:
        value = lax.pmax(value, axis)
    return value


def from_everyone(value, axis):
    devices = lax.axis_size(axis)
    return lax.all_to_all(
        jnp.broadcast_to(value[None], (devices, *value.shape)), axis, 0, 0, tiled=True
    )


def taken_together(value, axis):
    everything = from_everyone(value, axis)
    return jnp.max(everything, axis=0)


def rescale(scale, largest):
    return scale / jnp.sqrt(largest)


def on_device(tiles, tile_brow, tile_bcol, tile_count):
    slots = tiles.shape[2]
    width = tiles.shape[3]
    col_blocks = BR_DEV * lax.axis_size("prow") // lax.axis_size(PCOL)
    brow = tile_brow.reshape(slots)
    bcol = tile_bcol.reshape(slots)
    alive = (jnp.arange(slots, dtype=jnp.int32) < tile_count.reshape(1)).astype(jnp.float32)
    block = tiles.reshape(slots, width, width)
    row_vec = jnp.ones((BR_DEV, width), jnp.float32)
    col_vec = jnp.ones((col_blocks, width), jnp.float32)
    for sweep in range(SWEEPS):
        scaled = (
            jnp.abs(block.astype(jnp.float32))
            * row_vec[brow][:, :, None]
            * col_vec[bcol][:, None, :]
        )
        row_part = jnp.max(scaled, axis=2) * alive[:, None]
        col_part = jnp.max(scaled, axis=1) * alive[:, None]
        row_local = jnp.zeros((BR_DEV, width), jnp.float32).at[brow].max(row_part)
        col_local = jnp.zeros((col_blocks, width), jnp.float32).at[bcol].max(col_part)
        row_max = one_axis_at_a_time(row_local, PCOL)
        col_max = taken_together(col_local, "prow")
        row_vec = rescale(row_vec, row_max)
        col_vec = rescale(col_vec, col_max)
    return (row_vec.reshape(BR_DEV, 1, width), col_vec.reshape(col_blocks, 1, width))


def solution(mesh):
    finer = Mesh(mesh.devices.reshape(mesh.shape["prow"], 8, 4), ("prow", "pcol_0", "pcol_1"))
    in_specs = (
        P("prow", PCOL, None, None, None),
        P("prow", PCOL, None),
        P("prow", PCOL, None),
        P("prow", PCOL),
    )
    out_specs = (P(None, "prow", None), P(None, PCOL, None))
    return jax.shard_map(
        on_device, mesh=finer, in_specs=in_specs, out_specs=out_specs, check_vma=False
    )
```

profile of v0, /device:TPU:64, one launch (start us, length us, event | category | flops | bytes accessed | tf_op | source)
XLA Modules:
  0.0 187.4 jit_solution(17565205156358958719)
XLA Ops:
  0.6 0.7 fusion.33
  1.3 0.7 fusion.34
  3.9 5.1 %fusion.8 = (f32[32,256]{1,0:T(8,128)S(1)}, f32[32,256]{1,0:T(8,128)S(1)}) fusion(bf16[1,1,32,256,256]{4,3,2,1,0:T(8,128)(2,1)} %param.4, f32[32,256]{1,0:T(8,128)S(1)} %gather_fusion.1, f32[32,256]{1,0:T(8,128)S(1)} %gather_fusion), kind=kLoop, calls=%fused_computation.24 | loop fusion | flops 12566528 | bytes 4325376 | tf_op jit(solution)/shard_map/reduce_max | solution.py:50
  9.0 0.8 scatter_custom_fusion.1
  9.8 0.7 broadcast_in_dim.12
  10.5 10.0 %all-to-all-start = ((f32[16,16,256]{2,1,0:T(8,128)}), f32[16,16,256]{2,1,0:T(8,128)S(1)}, u32[]{:S(2)}, u32[]{:S(2)}) async-start(f32[16,16,256]{2,1,0:T(8,128)} %broadcast_in_dim.12), calls=%async_computation | async-start | bytes 524288 | tf_op jit(solution)/shard_map/all_to_all | solution.py:20
  20.5 0.8 scatter_custom_fusion
  21.3 30.4 %pmax.42 = f32[32,256]{1,0:T(8,128)S(1)} all-reduce(f32[32,256]{1,0:T(8,128)S(1)} %scatter_custom_fusion), channel_id=1, replica_groups=mesh['prow'=16,'pcol_0'=8,'pcol_1'=4] {'pcol_0'}, use_global_device_ids=true, to_apply=%region_2.0 | all-reduce | flops 8192 | bytes 65536 | tf_op jit(solution)/shard_map/pmax | solution.py:14
  51.7 17.1 %pmax.43 = f32[32,256]{1,0:T(8,128)S(1)} all-reduce(f32[32,256]{1,0:T(8,128)S(1)} %pmax.42), channel_id=1, replica_groups=mesh['prow'=16,'pcol_0'=8,'pcol_1'=4] {'pcol_1'}, use_global_device_ids=true, to_apply=%region_3.0 | all-reduce | flops 8192 | bytes 65536 | tf_op jit(solution)/shard_map/pmax | solution.py:14
  70.0 5.1 %fusion.5 = (f32[32,256]{1,0:T(8,128)S(1)}, f32[32,256]{1,0:T(8,128)S(1)}) fusion(bf16[1,1,32,256,256]{4,3,2,1,0:T(8,128)(2,1)} %param.4, f32[32,256]{1,0:T(8,128)S(1)} %gather_fusion.3, f32[32,256]{1,0:T(8,128)S(1)} %gather_fusion.2), kind=kLoop, calls=%fused_computation.21 | loop fusion | flops 12566528 | bytes 4325376 | tf_op jit(solution)/shard_map/reduce_max | solution.py:51
  75.2 0.8 scatter_custom_fusion.3
  76.0 0.7 broadcast_in_dim.13
  76.7 7.2 %all-to-all-start.1 = ((f32[16,16,256]{2,1,0:T(8,128)}), f32[16,16,256]{2,1,0:T(8,128)S(1)}, u32[]{:S(2)}, u32[]{:S(2)}) async-start(f32[16,16,256]{2,1,0:T(8,128)} %broadcast_in_dim.13), calls=%async_computation.1 | async-start | bytes 524288 | tf_op jit(solution)/shard_map/all_to_all | solution.py:20
  83.9 0.8 scatter_custom_fusion.2
  84.8 27.1 %pmax.44 = f32[32,256]{1,0:T(8,128)S(1)} all-reduce(f32[32,256]{1,0:T(8,128)S(1)} %scatter_custom_fusion.2), channel_id=1, replica_groups=mesh['prow'=16,'pcol_0'=8,'pcol_1'=4] {'pcol_0'}, use_global_device_ids=true, to_apply=%region_9.0 | all-reduce | flops 8192 | bytes 65536 | tf_op jit(solution)/shard_map/pmax | solution.py:14
  111.8 14.4 %pmax.45 = f32[32,256]{1,0:T(8,128)S(1)} all-reduce(f32[32,256]{1,0:T(8,128)S(1)} %pmax.44), channel_id=1, replica_groups=mesh['prow'=16,'pcol_0'=8,'pcol_1'=4] {'pcol_1'}, use_global_device_ids=true, to_apply=%region_10.0 | all-reduce | flops 8192 | bytes 65536 | tf_op jit(solution)/shard_map/pmax | solution.py:14
  127.6 5.1 %fusion.3 = (f32[32,256]{1,0:T(8,128)S(1)}, f32[32,256]{1,0:T(8,128)S(1)}) fusion(bf16[1,1,32,256,256]{4,3,2,1,0:T(8,128)(2,1)} %param.4, f32[32,256]{1,0:T(8,128)S(1)} %gather_fusion.5, f32[32,256]{1,0:T(8,128)S(1)} %gather_fusion.4), kind=kLoop, calls=%fused_computation.19 | loop fusion | flops 12566528 | bytes 4325376 | tf_op jit(solution)/shard_map/reduce_max | solution.py:51
  132.7 0.8 scatter_custom_fusion.5
  133.5 0.7 broadcast_in_dim.14
  134.2 7.2 %all-to-all-start.2 = ((f32[16,16,256]{2,1,0:T(8,128)}), f32[16,16,256]{2,1,0:T(8,128)S(1)}, u32[]{:S(2)}, u32[]{:S(2)}) async-start(f32[16,16,256]{2,1,0:T(8,128)} %broadcast_in_dim.14), calls=%async_computation.2 | async-start | bytes 524288 | tf_op jit(solution)/shard_map/all_to_all | solution.py:20
  141.4 0.8 scatter_custom_fusion.4
  142.3 27.6 %pmax.46 = f32[32,256]{1,0:T(8,128)S(1)} all-reduce(f32[32,256]{1,0:T(8,128)S(1)} %scatter_custom_fusion.4), channel_id=1, replica_groups=mesh['prow'=16,'pcol_0'=8,'pcol_1'=4] {'pcol_0'}, use_global_device_ids=true, to_apply=%region_16.0 | all-reduce | flops 8192 | bytes 65536 | tf_op jit(solution)/shard_map/pmax | solution.py:14
  169.8 16.2 %pmax.47 = f32[32,256]{1,0:T(8,128)S(1)} all-reduce(f32[32,256]{1,0:T(8,128)S(1)} %pmax.46), channel_id=1, replica_groups=mesh['prow'=16,'pcol_0'=8,'pcol_1'=4] {'pcol_1'}, use_global_device_ids=true, to_apply=%region_17.0 | all-reduce | flops 8192 | bytes 65536 | tf_op jit(solution)/shard_map/pmax | solution.py:14
  186.1 0.6 copy.8
  (24 shorter events, 4.4 us)
Async XLA Ops:
  10.5 58.9 %all-to-all-start = ((f32[16,16,256]{2,1,0:T(8,128)}), f32[16,16,256]{2,1,0:T(8,128)S(1)}, u32[]{:S(2)}, u32[]{:S(2)}) async-start(f32[16,16,256]{2,1,0:T(8,128)} %broadcast_in_dim.12), calls=%async_computation | async-start | bytes 524288 | tf_op jit(solution)/shard_map/all_to_all | solution.py:20
  76.7 50.2 %all-to-all-start.1 = ((f32[16,16,256]{2,1,0:T(8,128)}), f32[16,16,256]{2,1,0:T(8,128)S(1)}, u32[]{:S(2)}, u32[]{:S(2)}) async-start(f32[16,16,256]{2,1,0:T(8,128)} %broadcast_in_dim.13), calls=%async_computation.1 | async-start | bytes 524288 | tf_op jit(solution)/shard_map/all_to_all | solution.py:20
  134.2 52.5 %all-to-all-start.2 = ((f32[16,16,256]{2,1,0:T(8,128)}), f32[16,16,256]{2,1,0:T(8,128)S(1)}, u32[]{:S(2)}, u32[]{:S(2)}) async-start(f32[16,16,256]{2,1,0:T(8,128)} %broadcast_in_dim.14), calls=%async_computation.2 | async-start | bytes 524288 | tf_op jit(solution)/shard_map/all_to_all | solution.py:20
where the time goes:
time: 188 us; the launch traced here: 187 us
  blocking collectives  133 us (71%)
  starting transfers between devices  24.4 us (13%)
  other arithmetic  21.7 us (12%)
  local copies, waits for them, and re-layouts  7.07 us (4%)
    pmax x6, blocking collectives, one_axis_at_a_time(): value = lax.pmax(value, axis)  133 us
    all_to_all x3, starting transfers between devices, from_everyone(): lax.all_to_all(jnp.broadcast_to(value[None], (devices, *value.shape)), ax...  24.4 us
    reduce_max x2, other arithmetic, on_device(): col_part = jnp.max(scaled, axis=1) * alive[:, None]  10.2 us
    reduce_max x1, other arithmetic, on_device(): row_part = jnp.max(scaled, axis=2) * alive[:, None]  5.1 us
  transfers between devices with their start and end apart: 3, of which 0 were waited for; matrix products, arithmetic and copies ran while one was open for 2% of the time, Pallas kernels for 0%

commit v1 on v0

v1 whole, which is shorter than its diff:
```python
import functools

import jax
import jax.numpy as jnp
from jax import lax
from jax.experimental import pallas as pl
from jax.experimental.pallas import tpu as pltpu
from jax.sharding import PartitionSpec as P

MESH = pl.DeviceIdType.MESH
SWEEPS = 3
NX, NY, NZ, NC = 4, 8, 8, 2
PIECES, BLOCKS = 4, 8
LIFT = 2.0**63
KNEE = 2.0**64


def kernel(
    count_ref, brow_ref, bcol_ref, tiles_hbm, row_ref, col_ref,
    tiles, turned, row_u, row_v, col_u, col_v,
    rs_src, rs_got, plane, along, pair_src, pair_got,
    load_sem, send_sem, rs_sem, plane_sem, along_sem, pair_sem,
):
    slots, width = tiles.shape[0], tiles.shape[1]
    half = width // 2
    brs, bcs = row_ref.shape[0], col_ref.shape[0]
    piece = brs // PIECES
    prow, pcol = lax.axis_index("prow"), lax.axis_index("pcol")
    z, core = prow // NC, prow % NC
    y, x = pcol // NX, pcol % NX
    part = (y % 2) * 2 + x % 2
    block = (y // 2) * 2 + x // 2
    mine = part * BLOCKS + block

    loads = [
        pltpu.make_async_copy(tiles_hbm.at[s], tiles.at[s], load_sem.at[s])
        for s in range(slots)
    ]
    for load in loads:
        load.start()

    near = []
    for d in range(1, 4):
        px = x + (1 - 2 * (x % 2)) * (d % 2)
        py = y + (1 - 2 * (y % 2)) * (d // 2)
        near.append(((py % 2) * 2 + px % 2, (prow, py * NX + px)))
    offsets = [(dy, dx) for dy in range(NY) for dx in range(NX) if (dy, dx) != (0, 0)]
    offsets.sort(key=lambda o: -(min(o[0], NY - o[0]) + min(o[1], NX - o[1])))
    flat = [
        (prow, lax.rem(y + dy, NY) * NX + lax.rem(x + dx, NX)) for dy, dx in offsets
    ]
    steps = sorted(range(1, NZ), key=lambda d: -min(d, NZ - d))
    up = [(lax.rem(z + d, NZ) * NC + core, pcol) for d in steps]
    partner = (z * NC + 1 - core, pcol)

    barrier = pltpu.get_barrier_semaphore()
    everyone = flat + up + [partner]
    for device in everyone:
        pl.semaphore_signal(barrier, inc=1, device_id=device, device_id_type=MESH)

    count = count_ref[0]
    row_iota = lax.broadcasted_iota(jnp.int32, (brs, width), 0)
    col_iota = lax.broadcasted_iota(jnp.int32, (bcs, width), 0)

    def put(total, iota, where_to, s, value):
        place = jnp.where(s < count, where_to, -1)
        return jnp.maximum(total, jnp.where(iota == place, value, 0.0))

    def first(s, totals):
        rows, cols = totals
        tile = jnp.abs(tiles[s])
        tiles[s] = tile
        flip = tile.T
        turned[s] = flip
        rows = put(rows, row_iota, brow_ref[s], s, jnp.max(flip, axis=0, keepdims=True).astype(jnp.float32))
        cols = put(cols, col_iota, bcol_ref[s], s, jnp.max(tile, axis=0, keepdims=True).astype(jnp.float32))
        return rows, cols

    totals = (jnp.zeros((brs, width), jnp.float32), jnp.zeros((bcs, width), jnp.float32))
    for s in range(slots):
        loads[s].wait()
        totals = first(s, totals)
    rows, cols = totals

    def copy(src, dst, sem, device):
        pltpu.make_async_remote_copy(
            src_ref=src, dst_ref=dst, send_sem=send_sem, recv_sem=sem,
            device_id=device, device_id_type=MESH,
        ).start()

    def took(ref, sem):
        pltpu.make_async_copy(ref, ref, sem).wait()

    def row_scatter(sweep, value):
        rs_src[sweep] = value
        for d, (k, device) in enumerate(near):
            copy(rs_src.at[sweep, pl.ds(pl.multiple_of(k * piece, piece), piece)],
                 rs_got.at[sweep, d], rs_sem.at[sweep], device)

    def row_spread(sweep):
        took(rs_got.at[sweep], rs_sem.at[sweep])
        value = rs_src[sweep, pl.ds(pl.multiple_of(part * piece, piece), piece)]
        for d in range(3):
            value = jnp.maximum(value, rs_got[sweep, d])
        plane[sweep, mine] = value
        for device in flat:
            copy(plane.at[sweep, mine], plane.at[sweep, mine], plane_sem.at[sweep], device)

    def row_result(sweep):
        took(plane.at[sweep, pl.ds(0, len(flat))], plane_sem.at[sweep])
        pieces = []
        for k in range(PIECES):
            value = plane[sweep, k * BLOCKS]
            for b in range(1, BLOCKS):
                value = jnp.maximum(value, plane[sweep, k * BLOCKS + b])
            pieces.append(value)
        return jnp.concatenate(pieces, axis=0)

    def col_spread(sweep, value):
        along[sweep, z] = value
        for device in up:
            copy(along.at[sweep, z], along.at[sweep, z], along_sem.at[sweep], device)

    def col_swap(sweep):
        took(along.at[sweep, pl.ds(0, len(up))], along_sem.at[sweep])
        value = along[sweep, 0]
        for d in range(1, NZ):
            value = jnp.maximum(value, along[sweep, d])
        pair_src[sweep] = value
        copy(pair_src.at[sweep], pair_got.at[sweep], pair_sem.at[sweep], partner)

    def col_result(sweep):
        took(pair_got.at[sweep], pair_sem.at[sweep])
        return jnp.maximum(pair_src[sweep], pair_got[sweep])

    def rescale(scale, largest, sweep):
        if sweep == 0:
            return 1.0 / jnp.sqrt(largest)
        return scale / jnp.sqrt((largest * scale) * (1.0 / LIFT))

    def factors(scale, u_ref, v_ref):
        low = jnp.minimum(scale, KNEE)
        u_ref[...] = low * LIFT
        v_ref[...] = scale / low

    def again(source, u_ref, v_ref, from_ref, to_ref, iota, split):
        def body(s, total):
            pick = from_ref[s]
            value = source[s].astype(jnp.float32) * u_ref[pl.ds(pick, 1), :]
            if split:
                value = value * v_ref[pl.ds(pick, 1), :]
            value = jnp.maximum(value[:, :half], value[:, half:])
            value = jnp.max(value.T, axis=0, keepdims=True)
            return put(total, iota, to_ref[s], s, value)

        return lax.fori_loop(0, slots, body, jnp.zeros(iota.shape, jnp.float32), unroll=4)

    def row_pass(split):
        return again(tiles, col_u, col_v, bcol_ref, brow_ref, row_iota, split)

    def col_pass(split):
        return again(turned, row_u, row_v, brow_ref, bcol_ref, col_iota, split)

    pl.semaphore_wait(barrier, len(everyone))
    row_scatter(0, rows)
    col_spread(0, cols)
    row_scale = col_scale = None
    for sweep in range(SWEEPS):
        row_spread(sweep)
        col_swap(sweep)
        new_col = rescale(col_scale, col_result(sweep), sweep)
        last = sweep == SWEEPS - 1
        if not last:
            factors(new_col, col_u, col_v)
            row_scatter(sweep + 1, row_pass(sweep > 0))
        new_row = rescale(row_scale, row_result(sweep), sweep)
        if not last:
            factors(new_row, row_u, row_v)
            col_spread(sweep + 1, col_pass(sweep > 0))
        row_scale, col_scale = new_row, new_col
    row_ref[...] = row_scale
    col_ref[...] = col_scale

    for sweep in range(SWEEPS):
        took(rs_got.at[sweep], send_sem)
        took(plane.at[sweep, pl.ds(0, len(flat))], send_sem)
        took(along.at[sweep, pl.ds(0, len(up))], send_sem)
        took(pair_got.at[sweep], send_sem)


def on_device(tiles, tile_brow, tile_bcol, tile_count):
    slots, width = tiles.shape[2], tiles.shape[3]
    brs = 32
    bcs = brs * (NZ * NC) // (NX * NY)
    piece = brs // PIECES
    f32 = jnp.float32
    smem = pl.BlockSpec(memory_space=pltpu.SMEM)
    vmem = pl.BlockSpec(memory_space=pltpu.VMEM)
    rows, cols = pl.pallas_call(
        kernel,
        out_shape=(
            jax.ShapeDtypeStruct((brs, width), f32),
            jax.ShapeDtypeStruct((bcs, width), f32),
        ),
        in_specs=[smem, smem, smem, pl.BlockSpec(memory_space=pl.ANY)],
        out_specs=(vmem, vmem),
        scratch_shapes=[
            pltpu.VMEM((slots, width, width), jnp.bfloat16),
            pltpu.VMEM((slots, width, width), jnp.bfloat16),
            pltpu.VMEM((brs, width), f32),
            pltpu.VMEM((brs, width), f32),
            pltpu.VMEM((bcs, width), f32),
            pltpu.VMEM((bcs, width), f32),
            pltpu.VMEM((SWEEPS, brs, width), f32),
            pltpu.VMEM((SWEEPS, 3, piece, width), f32),
            pltpu.VMEM((SWEEPS, PIECES * BLOCKS, piece, width), f32),
            pltpu.VMEM((SWEEPS, NZ, bcs, width), f32),
            pltpu.VMEM((SWEEPS, bcs, width), f32),
            pltpu.VMEM((SWEEPS, bcs, width), f32),
            pltpu.SemaphoreType.DMA((slots,)),
            pltpu.SemaphoreType.DMA,
            pltpu.SemaphoreType.DMA((SWEEPS,)),
            pltpu.SemaphoreType.DMA((SWEEPS,)),
            pltpu.SemaphoreType.DMA((SWEEPS,)),
            pltpu.SemaphoreType.DMA((SWEEPS,)),
        ],
        name="equilibrate",
        compiler_params=pltpu.CompilerParams(
            collective_id=0, has_side_effects=True, vmem_limit_bytes=32 * 1024 * 1024
        ),
    )(
        tile_count.reshape(1),
        tile_brow.reshape(slots),
        tile_bcol.reshape(slots),
        tiles.reshape(slots, width, width),
    )
    return rows.reshape(brs, 1, width), cols.reshape(bcs, 1, width)


def solution(mesh):
    in_specs = (
        P("prow", "pcol", None, None, None),
        P("prow", "pcol", None),
        P("prow", "pcol", None),
        P("prow", "pcol"),
    )
    out_specs = (P(None, "prow", None), P(None, "pcol", None))
    return jax.shard_map(
        on_device, mesh=mesh, in_specs=in_specs, out_specs=out_specs, check_vma=False
    )
```

time: 188 us -> 60.2 us (0.32)
  the two profiles are of different devices: /device:TPU:64 before, /device:TPU:1 now
where the time goes in v1:
time: 60.2 us; the launch traced here: 60 us
  Pallas kernels  54 us (90%)
  local copies, waits for them, and re-layouts  4.76 us (8%)
  between operations  1.3 us (2%)
    pallas_call x1, Pallas kernels, on_device(): pl.pallas_call(kernel, out_shape=(jax.ShapeDtypeStruct((brs, width), f32)...  54 us
    unnamed x8, local copies, waits for them, and re-layouts  4.76 us

profile of v1, /device:TPU:1, one launch (start us, length us, event | category | flops | bytes accessed | tf_op | source)
XLA Modules:
  0.0 60.0 jit_solution(10241279393665466695)
XLA Ops:
  1.3 0.0 copy-start
  1.3 2.2 %copy-done = bf16[1,1,32,256,256]{4,3,2,1,0:T(8,128)(2,1)S(1)} copy-done((bf16[1,1,32,256,256]{4,3,2,1,0:T(8,128)(2,1)S(1)}, bf16[1,1,32,256,256]{4,3,2,1,0:T(8,128)(2,1)}, u32[]{:S(2)}) %copy-start) | copy-done | bytes 4194328
  3.5 0.0 copy-start.1
  3.5 0.7 %copy-done.1 = s32[1,1,32]{2,1,0:T(1,128)S(1)} copy-done((s32[1,1,32]{2,1,0:T(1,128)S(1)}, s32[1,1,32]{2,1,0:T(1,128)}, u32[]{:S(2)}) %copy-start.1) | copy-done | bytes 152
  4.1 0.0 copy-start.2
  4.1 0.7 %copy-done.2 = s32[1,1,32]{2,1,0:T(1,128)S(1)} copy-done((s32[1,1,32]{2,1,0:T(1,128)S(1)}, s32[1,1,32]{2,1,0:T(1,128)}, u32[]{:S(2)}) %copy-start.2) | copy-done | bytes 152
  4.8 54.0 %equilibrate.1 = (f32[32,256]{1,0:T(8,128)S(1)}, f32[16,256]{1,0:T(8,128)S(1)}) custom-call(s32[1]{0:T(128)} %bitcast.6.count_ref, s32[32]{0:T(128)S(1)} %bitcast.10, s32[32]{0:T(128)S(1)} %bitcast.11, bf16[32,256,256]{2,1,0:T(8,128)(2,1)S(1)} %bitcast.7), custom_call_target="tpu_custom_call" | custom-call | tf_op jit(solution)/shard_map/equilibrate/pallas_call | solution.py:199
  58.8 0.6 %copy.6 = f32[32,1,256]{2,1,0:T(1,128)} copy(f32[32,1,256]{2,0,1:T(8,128)S(1)} %bitcast.8) | data formatting | bytes 65536
  59.4 0.6 %copy.7 = f32[16,1,256]{2,1,0:T(1,128)} copy(f32[16,1,256]{2,0,1:T(8,128)S(1)} %bitcast.9) | data formatting | bytes 32768
Async XLA Ops:
  1.3 2.2 %copy-start = (bf16[1,1,32,256,256]{4,3,2,1,0:T(8,128)(2,1)S(1)}, bf16[1,1,32,256,256]{4,3,2,1,0:T(8,128)(2,1)}, u32[]{:S(2)}) copy-start(bf16[1,1,32,256,256]{4,3,2,1,0:T(8,128)(2,1)} %param.4) | copy-start | bytes 12582916
  3.5 0.7 %copy-start.1 = (s32[1,1,32]{2,1,0:T(1,128)S(1)}, s32[1,1,32]{2,1,0:T(1,128)}, u32[]{:S(2)}) copy-start(s32[1,1,32]{2,1,0:T(1,128)} %param.5) | copy-start | bytes 388
  4.1 0.7 %copy-start.2 = (s32[1,1,32]{2,1,0:T(1,128)S(1)}, s32[1,1,32]{2,1,0:T(1,128)}, u32[]{:S(2)}) copy-start(s32[1,1,32]{2,1,0:T(1,128)} %param.6) | copy-start | bytes 388

commit v2 on v1

v2 whole, which is shorter than its diff:
```python
import functools

import jax
import jax.numpy as jnp
from jax import lax
from jax.experimental import pallas as pl
from jax.experimental.pallas import tpu as pltpu
from jax.sharding import PartitionSpec as P

MESH = pl.DeviceIdType.MESH
SWEEPS = 3
NX, NY, NZ, NC = 4, 8, 8, 2
PIECES, BLOCKS = 8, 4
REACH = 2
CHUNK = 4
VMEM_LIMIT = 32 * 1024 * 1024
UNROLL = 16
LIFT = 2.0**63
KNEE = 2.0**64


def kernel(
    count_ref, brow_hbm, bcol_hbm, tiles_hbm, row_ref, col_ref,
    brow_smem, bcol_smem, tiles, turned, row_u, row_v, col_u, col_v,
    rs_src, rs_got, plane, along, pair_src, pair_got,
    enter_sem, index_sem, load_sem, send_sem, rs_sem, plane_sem, along_sem, pair_sem,
):
    slots, width = tiles.shape[0], tiles.shape[1]
    half = width // 2
    brs, bcs = row_ref.shape[0], col_ref.shape[0]
    piece = brs * 2 // PIECES
    prow, pcol = lax.axis_index("prow"), lax.axis_index("pcol")
    z, core = prow // NC, prow % NC
    y, x = pcol // NX, pcol % NX
    part = (y % 2) * NX + x
    block = y // 2
    mine = part * BLOCKS + block

    indices = [
        pltpu.make_async_copy(src, dst, index_sem.at[i])
        for i, (src, dst) in enumerate(
            ((brow_hbm, brow_smem), (bcol_hbm, bcol_smem))
        )
    ]
    loads = [
        pltpu.make_async_copy(
            tiles_hbm.at[0, 0, pl.ds(c * CHUNK, CHUNK)],
            tiles.at[pl.ds(c * CHUNK, CHUNK)], load_sem.at[c],
        )
        for c in range(slots // CHUNK)
    ]
    for load in loads + indices:
        load.start()

    near = []
    for d in range(1, PIECES):
        px = lax.rem(x + d, NX)
        py = y + (1 - 2 * (y % 2)) * (d // NX)
        near.append(((py % 2) * NX + px, (prow, py * NX + px)))
    beyond = [(prow, lax.rem(y + d, NY) * NX + x) for d in (REACH, NY - REACH)]
    offsets = [(dy, dx) for dy in range(NY) for dx in range(NX) if (dy, dx) != (0, 0)]
    offsets.sort(key=lambda o: -(min(o[0], NY - o[0]) + min(o[1], NX - o[1])))
    flat = [
        (prow, lax.rem(y + dy, NY) * NX + lax.rem(x + dx, NX)) for dy, dx in offsets
    ]
    steps = sorted(range(1, NZ), key=lambda d: -min(d, NZ - d))
    up = [(lax.rem(z + d, NZ) * NC + core, pcol) for d in steps]
    partner = (z * NC + 1 - core, pcol)

    barrier = pltpu.get_barrier_semaphore()
    everyone = [device for _, device in near] + beyond + up + [partner]
    for device in everyone:
        pl.semaphore_signal(barrier, inc=1, device_id=device, device_id_type=MESH)

    with jax.named_scope("index"):
        for load in indices:
            load.wait()
    count = count_ref[0]
    brow_ref, bcol_ref = brow_smem.at[0, 0], bcol_smem.at[0, 0]
    row_iota = lax.broadcasted_iota(jnp.int32, (brs, width), 0)
    col_iota = lax.broadcasted_iota(jnp.int32, (bcs, width), 0)

    def put(total, iota, where_to, s, value):
        place = jnp.where(s < count, where_to, -1)
        return jnp.maximum(total, jnp.where(iota == place, value, 0.0))

    def first(c, totals):
        rows, cols = totals
        pltpu.make_async_copy(
            tiles_hbm.at[0, 0, pl.ds(c * CHUNK, CHUNK)],
            tiles.at[pl.ds(c * CHUNK, CHUNK)], load_sem.at[c],
        ).wait()
        for i in range(CHUNK):
            s = c * CHUNK + i
            tile = jnp.abs(tiles[s])
            tiles[s] = tile
            fold = jnp.maximum(tile[:, :half], tile[:, half:]).T
            row = jnp.max(fold, axis=0, keepdims=True).astype(jnp.float32)
            col = jnp.max(tile, axis=0, keepdims=True).astype(jnp.float32)
            rows = put(rows, row_iota, brow_ref[s], s, row)
            cols = put(cols, col_iota, bcol_ref[s], s, col)
        return rows, cols

    totals = (jnp.zeros((brs, width), jnp.float32), jnp.zeros((bcs, width), jnp.float32))
    with jax.named_scope("first"):
        rows, cols = lax.fori_loop(0, slots // CHUNK, first, totals)

    def turn(s, _):
        turned[s] = tiles[s].T
        return 0

    def copy(src, dst, sem, device):
        pltpu.make_async_remote_copy(
            src_ref=src, dst_ref=dst, send_sem=send_sem, recv_sem=sem,
            device_id=device, device_id_type=MESH,
        ).start()

    def took(ref, sem):
        pltpu.make_async_copy(ref, ref, sem).wait()

    def spot(k):
        return (
            pl.ds(pl.multiple_of(k // 2 * piece, piece), piece),
            pl.ds(pl.multiple_of(k % 2 * half, half), half),
        )

    def row_scatter(sweep, value):
        rs_src[sweep] = value
        for d, (k, device) in enumerate(near):
            copy(rs_src.at[(sweep, *spot(k))], rs_got.at[sweep, d], rs_sem.at[sweep], device)

    def row_spread(sweep):
        with jax.named_scope("rs_wait"):
            took(rs_got.at[sweep], rs_sem.at[sweep])
        value = rs_src[(sweep, *spot(part))]
        for d in range(len(near)):
            value = jnp.maximum(value, rs_got[sweep, d])
        plane[sweep, mine] = value
        for device in flat:
            copy(plane.at[sweep, mine], plane.at[sweep, mine], plane_sem.at[sweep], device)

    def row_result(sweep):
        with jax.named_scope("plane_wait"):
            took(plane.at[sweep, pl.ds(0, len(flat))], plane_sem.at[sweep])
        pieces = []
        for k in range(PIECES):
            value = plane[sweep, k * BLOCKS]
            for b in range(1, BLOCKS):
                value = jnp.maximum(value, plane[sweep, k * BLOCKS + b])
            pieces.append(value)
        return jnp.concatenate(
            [jnp.concatenate(pieces[k : k + 2], axis=1) for k in range(0, PIECES, 2)],
            axis=0,
        )

    def col_spread(sweep, value):
        along[sweep, z] = value
        for device in up:
            copy(along.at[sweep, z], along.at[sweep, z], along_sem.at[sweep], device)

    def col_swap(sweep):
        with jax.named_scope("along_wait"):
            took(along.at[sweep, pl.ds(0, len(up))], along_sem.at[sweep])
        value = along[sweep, 0]
        for d in range(1, NZ):
            value = jnp.maximum(value, along[sweep, d])
        pair_src[sweep] = value
        copy(pair_src.at[sweep], pair_got.at[sweep], pair_sem.at[sweep], partner)

    def col_result(sweep):
        with jax.named_scope("pair_wait"):
            took(pair_got.at[sweep], pair_sem.at[sweep])
        return jnp.maximum(pair_src[sweep], pair_got[sweep])

    def rescale(scale, largest, sweep):
        if sweep == 0:
            return 1.0 / jnp.sqrt(largest)
        return scale / jnp.sqrt((largest * scale) * (1.0 / LIFT))

    def factors(scale, u_ref, v_ref):
        low = jnp.minimum(scale, KNEE)
        u_ref[...] = low * LIFT
        v_ref[...] = scale / low

    def again(source, u_ref, v_ref, from_ref, to_ref, iota, split):
        def body(s, total):
            pick = from_ref[s]
            value = source[s].astype(jnp.float32) * u_ref[pl.ds(pick, 1), :]
            if split:
                value = value * v_ref[pl.ds(pick, 1), :]
            value = jnp.maximum(value[:, :half], value[:, half:])
            value = jnp.max(value.T, axis=0, keepdims=True)
            return put(total, iota, to_ref[s], s, value)

        return lax.fori_loop(0, slots, body, jnp.zeros(iota.shape, jnp.float32), unroll=UNROLL)

    def row_pass(split):
        return again(tiles, col_u, col_v, bcol_ref, brow_ref, row_iota, split)

    def col_pass(split):
        return again(turned, row_u, row_v, brow_ref, bcol_ref, col_iota, split)

    with jax.named_scope("enter"):
        pl.semaphore_wait(barrier, len(everyone))
    row_scatter(0, rows)
    col_spread(0, cols)
    for stage in range(2):
        for device in beyond:
            pl.semaphore_signal(
                enter_sem.at[stage], inc=1, device_id=device, device_id_type=MESH
            )
        with jax.named_scope("turn"):
            lax.fori_loop(stage * slots // 2, (stage + 1) * slots // 2, turn, 0, unroll=8)
        with jax.named_scope("stage"):
            pl.semaphore_wait(enter_sem.at[stage], len(beyond))
    row_scale = col_scale = None
    for sweep in range(SWEEPS):
        row_spread(sweep)
        col_swap(sweep)
        new_col = rescale(col_scale, col_result(sweep), sweep)
        last = sweep == SWEEPS - 1
        if not last:
            factors(new_col, col_u, col_v)
            with jax.named_scope("row_pass"):
                value = row_pass(sweep > 0)
            row_scatter(sweep + 1, value)
        new_row = rescale(row_scale, row_result(sweep), sweep)
        if not last:
            factors(new_row, row_u, row_v)
            with jax.named_scope("col_pass"):
                value = col_pass(sweep > 0)
            col_spread(sweep + 1, value)
        row_scale, col_scale = new_row, new_col
    row_ref[...] = row_scale.reshape(row_ref.shape)
    col_ref[...] = col_scale.reshape(col_ref.shape)

    with jax.named_scope("drain"):
        for sweep in range(SWEEPS):
            took(rs_got.at[sweep], send_sem)
            took(plane.at[sweep, pl.ds(0, len(flat))], send_sem)
            took(along.at[sweep, pl.ds(0, len(up))], send_sem)
            took(pair_got.at[sweep], send_sem)


def finish(rows, cols, row_ref, col_ref):
    row_ref[...] = rows[...]
    col_ref[...] = cols[...]


def on_device(tiles, tile_brow, tile_bcol, tile_count):
    slots, width = tiles.shape[2], tiles.shape[3]
    brs = 32
    bcs = brs * (NZ * NC) // (NX * NY)
    piece, half = brs * 2 // PIECES, width // 2
    f32 = jnp.float32
    vmem = pl.BlockSpec(memory_space=pltpu.VMEM)
    rows, cols = pl.pallas_call(
        kernel,
        out_shape=(
            jax.ShapeDtypeStruct((brs, 1, width), f32),
            jax.ShapeDtypeStruct((bcs, 1, width), f32),
        ),
        in_specs=[pl.BlockSpec(memory_space=pltpu.SMEM)] + [pl.BlockSpec(memory_space=pltpu.HBM)] * 3,
        out_specs=(vmem, vmem),
        scratch_shapes=[
            pltpu.SMEM((1, 1, slots), jnp.int32),
            pltpu.SMEM((1, 1, slots), jnp.int32),
            pltpu.VMEM((slots, width, width), jnp.bfloat16),
            pltpu.VMEM((slots, width, width), jnp.bfloat16),
            pltpu.VMEM((brs, width), f32),
            pltpu.VMEM((brs, width), f32),
            pltpu.VMEM((bcs, width), f32),
            pltpu.VMEM((bcs, width), f32),
            pltpu.VMEM((SWEEPS, brs, width), f32),
            pltpu.VMEM((SWEEPS, PIECES - 1, piece, half), f32),
            pltpu.VMEM((SWEEPS, PIECES * BLOCKS, piece, half), f32),
            pltpu.VMEM((SWEEPS, NZ, bcs, width), f32),
            pltpu.VMEM((SWEEPS, bcs, width), f32),
            pltpu.VMEM((SWEEPS, bcs, width), f32),
            pltpu.SemaphoreType.REGULAR((2,)),
            pltpu.SemaphoreType.DMA((2,)),
            pltpu.SemaphoreType.DMA((slots // CHUNK,)),
            pltpu.SemaphoreType.DMA,
            pltpu.SemaphoreType.DMA((SWEEPS,)),
            pltpu.SemaphoreType.DMA((SWEEPS,)),
            pltpu.SemaphoreType.DMA((SWEEPS,)),
            pltpu.SemaphoreType.DMA((SWEEPS,)),
        ],
        name="equilibrate",
        compiler_params=pltpu.CompilerParams(
            collective_id=0, has_side_effects=True, vmem_limit_bytes=VMEM_LIMIT
        ),
    )(
        tile_count.reshape(1),
        *(
            pltpu.with_memory_space_constraint(a, pltpu.HBM)
            for a in (tile_brow, tile_bcol, tiles)
        ),
    )
    return rows, cols
    return pl.pallas_call(
        finish,
        out_shape=(
            jax.ShapeDtypeStruct(rows.shape, f32),
            jax.ShapeDtypeStruct(cols.shape, f32),
        ),
        in_specs=[vmem, vmem],
        out_specs=(vmem, vmem),
        name="finish",
    )(rows, cols)


def solution(mesh):
    in_specs = (
        P("prow", "pcol", None, None, None),
        P("prow", "pcol", None),
        P("prow", "pcol", None),
        P("prow", "pcol"),
    )
    out_specs = (P(None, "prow", None), P(None, "pcol", None))
    return jax.shard_map(
        on_device, mesh=mesh, in_specs=in_specs, out_specs=out_specs, check_vma=False
    )
```

time: 60.2 us -> 46.2 us (0.77)
  Pallas kernels: 54 us -> 43.6 us
  local copies, waits for them, and re-layouts: 4.76 us -> 1.22 us
    pallas_call x1, Pallas kernels: 54 us -> 43.6 us  [on_device(): pl.pallas_call(kernel, out_shape=(jax.ShapeDtypeStruct((brs, 1, width), f...]
    unnamed x8 -> x2, local copies, waits for them, and re-layouts: 4.76 us -> 1.22 us
where the time goes in v2:
time: 46.2 us; the launch traced here: 46.1 us
  Pallas kernels  43.6 us (94%)
  between operations  1.29 us (3%)
  local copies, waits for them, and re-layouts  1.22 us (3%)
    pallas_call x1, Pallas kernels, on_device(): pl.pallas_call(kernel, out_shape=(jax.ShapeDtypeStruct((brs, 1, width), f...  43.6 us
    unnamed x2, local copies, waits for them, and re-layouts  1.22 us

profile of v2, /device:TPU:1, one launch (start us, length us, event | category | flops | bytes accessed | tf_op | source)
XLA Modules:
  0.0 46.1 jit_solution(12269827281812196587)
XLA Ops:
  1.3 43.6 %equilibrate.1 = (f32[32,1,256]{2,1,0:T(1,128)S(1)}, f32[16,1,256]{2,1,0:T(1,128)S(1)}) custom-call(s32[1]{0:T(128)} %bitcast.1.count_ref, s32[1,1,32]{2,1,0:T(1,128)} %brow_hbm.1, s32[1,1,32]{2,1,0:T(1,128)} %bcol_hbm.1, bf16[1,1,32,256,256]{4,3,2,1,0:T(8,128)(2,1)} %tiles_hbm.1), custom_call_target="tpu_custom_call" | custom-call | tf_op jit(solution)/shard_map/equilibrate/pallas_call | solution.py:257
  44.9 0.6 %copy.9 = f32[32,1,256]{2,1,0:T(1,128)} copy(f32[32,1,256]{2,1,0:T(1,128)S(1)} %get-tuple-element.4) | data formatting | bytes 65536
  45.5 0.6 %copy.10 = f32[16,1,256]{2,1,0:T(1,128)} copy(f32[16,1,256]{2,1,0:T(1,128)S(1)} %get-tuple-element.5) | data formatting | bytes 32768

commit v3 on v2

--- a/solution.py
+++ b/solution.py
@@ -11,10 +11,10 @@
 SWEEPS = 3
 NX, NY, NZ, NC = 4, 8, 8, 2
 PIECES, BLOCKS = 8, 4
-REACH = 2
+REACHES = (1, 2)
 CHUNK = 4
 VMEM_LIMIT = 32 * 1024 * 1024
-UNROLL = 16
+UNROLL = 32
 LIFT = 2.0**63
 KNEE = 2.0**64
 
@@ -57,7 +57,14 @@
         px = lax.rem(x + d, NX)
         py = y + (1 - 2 * (y % 2)) * (d // NX)
         near.append(((py % 2) * NX + px, (prow, py * NX + px)))
-    beyond = [(prow, lax.rem(y + d, NY) * NX + x) for d in (REACH, NY - REACH)]
+    greet = [
+        (prow, lax.rem(y + dy, NY) * NX + lax.rem(x + dx, NX))
+        for dy in (1, NY - 1, 0) for dx in range(NX) if (dy, dx) != (0, 0)
+    ]
+    beyond = [
+        [(prow, lax.rem(y + d, NY) * NX + x) for d in (reach, NY - reach)]
+        for reach in REACHES
+    ]
     offsets = [(dy, dx) for dy in range(NY) for dx in range(NX) if (dy, dx) != (0, 0)]
     offsets.sort(key=lambda o: -(min(o[0], NY - o[0]) + min(o[1], NX - o[1])))
     flat = [
@@ -68,7 +75,7 @@
     partner = (z * NC + 1 - core, pcol)
 
     barrier = pltpu.get_barrier_semaphore()
-    everyone = [device for _, device in near] + beyond + up + [partner]
+    everyone = greet + up + [partner]
     for device in everyone:
         pl.semaphore_signal(barrier, inc=1, device_id=device, device_id_type=MESH)
 
@@ -204,15 +211,16 @@
         pl.semaphore_wait(barrier, len(everyone))
     row_scatter(0, rows)
     col_spread(0, cols)
-    for stage in range(2):
-        for device in beyond:
+    for stage, devices in enumerate(beyond):
+        for device in devices:
             pl.semaphore_signal(
                 enter_sem.at[stage], inc=1, device_id=device, device_id_type=MESH
             )
-        with jax.named_scope("turn"):
-            lax.fori_loop(stage * slots // 2, (stage + 1) * slots // 2, turn, 0, unroll=8)
+        if stage == len(beyond) - 1:
+            with jax.named_scope("turn"):
+                lax.fori_loop(0, slots, turn, 0, unroll=8)
         with jax.named_scope("stage"):
-            pl.semaphore_wait(enter_sem.at[stage], len(beyond))
+            pl.semaphore_wait(enter_sem.at[stage], len(devices))
     row_scale = col_scale = None
     for sweep in range(SWEEPS):
         row_spread(sweep)
@@ -242,9 +250,15 @@
             took(pair_got.at[sweep], send_sem)
 
 
-def finish(rows, cols, row_ref, col_ref):
-    row_ref[...] = rows[...]
-    col_ref[...] = cols[...]
+def finish(rows, cols, row_out, col_out, sem):
+    moves = [
+        pltpu.make_async_copy(src, dst, sem.at[i])
+        for i, (src, dst) in enumerate(((rows, row_out), (cols, col_out)))
+    ]
+    for move in moves:
+        move.start()
+    for move in moves:
+        move.wait()
 
 
 def on_device(tiles, tile_brow, tile_bcol, tile_count):
@@ -297,7 +311,7 @@
             for a in (tile_brow, tile_bcol, tiles)
         ),
     )
-    return rows, cols
+    anywhere = pl.BlockSpec(memory_space=pltpu.HBM)
     return pl.pallas_call(
         finish,
         out_shape=(
@@ -305,9 +319,10 @@
             jax.ShapeDtypeStruct(cols.shape, f32),
         ),
         in_specs=[vmem, vmem],
-        out_specs=(vmem, vmem),
+        out_specs=(anywhere, anywhere),
+        scratch_shapes=[pltpu.SemaphoreType.DMA((2,))],
         name="finish",
-    )(rows, cols)
+    )(*(pltpu.with_memory_space_constraint(a, pltpu.VMEM) for a in (rows, cols)))
 
 
 def solution(mesh):

time: 46.2 us -> 45.2 us (0.978)
  local copies, waits for them, and re-layouts: 1.22 us -> 0 us
    unnamed x2 -> x0, local copies, waits for them, and re-layouts: 1.22 us -> none
    pallas_call x0 -> x1, Pallas kernels: none -> 0.64 us  [on_device(): pl.pallas_call(finish, out_shape=(jax.ShapeDtypeStruct(rows.shape, f32),...]
    pallas_call x1, Pallas kernels: 43.6 us -> 43.1 us  [on_device(): pl.pallas_call(kernel, out_shape=(jax.ShapeDtypeStruct((brs, 1, width), f...]
where the time goes in v3:
time: 45.2 us; the launch traced here: 45.1 us
  Pallas kernels  43.8 us (97%)
  between operations  1.29 us (3%)
    pallas_call x1, Pallas kernels, on_device(): pl.pallas_call(kernel, out_shape=(jax.ShapeDtypeStruct((brs, 1, width), f...  43.1 us

profile of v3, /device:TPU:1, one launch (start us, length us, event | category | flops | bytes accessed | tf_op | source)
XLA Modules:
  0.0 45.1 jit_solution(17555450574707769326)
XLA Ops:
  1.3 43.1 %equilibrate.1 = (f32[32,1,256]{2,1,0:T(1,128)S(1)}, f32[16,1,256]{2,1,0:T(1,128)S(1)}) custom-call(s32[1]{0:T(128)} %bitcast.1.count_ref, s32[1,1,32]{2,1,0:T(1,128)} %brow_hbm.1, s32[1,1,32]{2,1,0:T(1,128)} %bcol_hbm.1, bf16[1,1,32,256,256]{4,3,2,1,0:T(8,128)(2,1)} %tiles_hbm.1), custom_call_target="tpu_custom_call" | custom-call | tf_op jit(solution)/shard_map/equilibrate/pallas_call | solution.py:271
  44.4 0.6 %finish.1 = (f32[32,1,256]{2,1,0:T(1,128)}, f32[16,1,256]{2,1,0:T(1,128)}) custom-call(f32[32,1,256]{2,1,0:T(1,128)S(1)} %get-tuple-element.4.rows, f32[16,1,256]{2,1,0:T(1,128)S(1)} %get-tuple-element.5.cols), custom_call_target="tpu_custom_call" | custom-call | tf_op jit(solution)/shard_map/finish/pallas_call | solution.py:315

commit v4 on v3

--- a/solution.py
+++ b/solution.py
@@ -10,7 +10,8 @@
 MESH = pl.DeviceIdType.MESH
 SWEEPS = 3
 NX, NY, NZ, NC = 4, 8, 8, 2
-PIECES, BLOCKS = 8, 4
+PAIRS = 4
+APART = (0, 1, 1, 2)
 REACHES = (1, 2)
 CHUNK = 4
 VMEM_LIMIT = 32 * 1024 * 1024
@@ -28,13 +29,10 @@
     slots, width = tiles.shape[0], tiles.shape[1]
     half = width // 2
     brs, bcs = row_ref.shape[0], col_ref.shape[0]
-    piece = brs * 2 // PIECES
+    piece = brs // NX
     prow, pcol = lax.axis_index("prow"), lax.axis_index("pcol")
     z, core = prow // NC, prow % NC
     y, x = pcol // NX, pcol % NX
-    part = (y % 2) * NX + x
-    block = y // 2
-    mine = part * BLOCKS + block
 
     indices = [
         pltpu.make_async_copy(src, dst, index_sem.at[i])
@@ -52,11 +50,19 @@
     for load in loads + indices:
         load.start()
 
-    near = []
-    for d in range(1, PIECES):
-        px = lax.rem(x + d, NX)
-        py = y + (1 - 2 * (y % 2)) * (d // NX)
-        near.append(((py % 2) * NX + px, (prow, py * NX + px)))
+    side = 2 * (y % 2) - 1
+    near, far = [], []
+    for turns in (1, 0):
+        for dx in (2, 1, 3, 0):
+            if (turns, dx) != (0, 0):
+                px = lax.rem(x + dx, NX)
+                near.append((px, (prow, (y - side * turns) * NX + px)))
+    for turns in (3, 2, 1, 0):
+        for dx in (2, 1, 3, 0):
+            if (turns, dx) != (0, 0):
+                py = lax.rem(y + NY + side * turns, NY)
+                slot = lax.rem(PAIRS - side * APART[turns], PAIRS)
+                far.append((slot, (prow, py * NX + lax.rem(x + dx, NX))))
     greet = [
         (prow, lax.rem(y + dy, NY) * NX + lax.rem(x + dx, NX))
         for dy in (1, NY - 1, 0) for dx in range(NX) if (dy, dx) != (0, 0)
@@ -64,11 +70,6 @@
     beyond = [
         [(prow, lax.rem(y + d, NY) * NX + x) for d in (reach, NY - reach)]
         for reach in REACHES
-    ]
-    offsets = [(dy, dx) for dy in range(NY) for dx in range(NX) if (dy, dx) != (0, 0)]
-    offsets.sort(key=lambda o: -(min(o[0], NY - o[0]) + min(o[1], NX - o[1])))
-    flat = [
-        (prow, lax.rem(y + dy, NY) * NX + lax.rem(x + dx, NX)) for dy, dx in offsets
     ]
     steps = sorted(range(1, NZ), key=lambda d: -min(d, NZ - d))
     up = [(lax.rem(z + d, NZ) * NC + core, pcol) for d in steps]
@@ -126,39 +127,33 @@
         pltpu.make_async_copy(ref, ref, sem).wait()
 
     def spot(k):
-        return (
-            pl.ds(pl.multiple_of(k // 2 * piece, piece), piece),
-            pl.ds(pl.multiple_of(k % 2 * half, half), half),
-        )
+        return pl.ds(pl.multiple_of(k * piece, piece), piece)
 
     def row_scatter(sweep, value):
         rs_src[sweep] = value
         for d, (k, device) in enumerate(near):
-            copy(rs_src.at[(sweep, *spot(k))], rs_got.at[sweep, d], rs_sem.at[sweep], device)
+            copy(rs_src.at[sweep, spot(k)], rs_got.at[sweep, d], rs_sem.at[sweep], device)
 
     def row_spread(sweep):
         with jax.named_scope("rs_wait"):
             took(rs_got.at[sweep], rs_sem.at[sweep])
-        value = rs_src[(sweep, *spot(part))]
+        value = rs_src[sweep, spot(x)]
         for d in range(len(near)):
             value = jnp.maximum(value, rs_got[sweep, d])
-        plane[sweep, mine] = value
-        for device in flat:
-            copy(plane.at[sweep, mine], plane.at[sweep, mine], plane_sem.at[sweep], device)
+        plane[sweep, x] = value
+        for slot, device in far:
+            copy(plane.at[sweep, x], plane.at[sweep, slot * NX + x], plane_sem.at[sweep], device)
 
     def row_result(sweep):
         with jax.named_scope("plane_wait"):
-            took(plane.at[sweep, pl.ds(0, len(flat))], plane_sem.at[sweep])
+            took(plane.at[sweep, pl.ds(0, len(far))], plane_sem.at[sweep])
         pieces = []
-        for k in range(PIECES):
-            value = plane[sweep, k * BLOCKS]
-            for b in range(1, BLOCKS):
-                value = jnp.maximum(value, plane[sweep, k * BLOCKS + b])
+        for k in range(NX):
+            value = plane[sweep, k]
+            for b in range(1, PAIRS):
+                value = jnp.maximum(value, plane[sweep, b * NX + k])
             pieces.append(value)
-        return jnp.concatenate(
-            [jnp.concatenate(pieces[k : k + 2], axis=1) for k in range(0, PIECES, 2)],
-            axis=0,
-        )
+        return jnp.concatenate(pieces, axis=0)
 
     def col_spread(sweep, value):
         along[sweep, z] = value
@@ -245,7 +240,7 @@
     with jax.named_scope("drain"):
         for sweep in range(SWEEPS):
             took(rs_got.at[sweep], send_sem)
-            took(plane.at[sweep, pl.ds(0, len(flat))], send_sem)
+            took(plane.at[sweep, pl.ds(0, len(far))], send_sem)
             took(along.at[sweep, pl.ds(0, len(up))], send_sem)
             took(pair_got.at[sweep], send_sem)
 
@@ -265,7 +260,7 @@
     slots, width = tiles.shape[2], tiles.shape[3]
     brs = 32
     bcs = brs * (NZ * NC) // (NX * NY)
-    piece, half = brs * 2 // PIECES, width // 2
+    piece = brs // NX
     f32 = jnp.float32
     vmem = pl.BlockSpec(memory_space=pltpu.VMEM)
     rows, cols = pl.pallas_call(
@@ -286,8 +281,8 @@
             pltpu.VMEM((bcs, width), f32),
             pltpu.VMEM((bcs, width), f32),
             pltpu.VMEM((SWEEPS, brs, width), f32),
-            pltpu.VMEM((SWEEPS, PIECES - 1, piece, half), f32),
-            pltpu.VMEM((SWEEPS, PIECES * BLOCKS, piece, half), f32),
+            pltpu.VMEM((SWEEPS, 2 * NX - 1, piece, width), f32),
+            pltpu.VMEM((SWEEPS, PAIRS * NX, piece, width), f32),
             pltpu.VMEM((SWEEPS, NZ, bcs, width), f32),
             pltpu.VMEM((SWEEPS, bcs, width), f32),
             pltpu.VMEM((SWEEPS, bcs, width), f32),

time: 45.2 us -> 44.1 us (0.976)
  Pallas kernels: 43.8 us -> 42.6 us
    pallas_call x1, Pallas kernels: 43.1 us -> 42 us  [on_device(): pl.pallas_call(kernel, out_shape=(jax.ShapeDtypeStruct((brs, 1, width), f...]
where the time goes in v4:
time: 44.1 us; the launch traced here: 43.9 us
  Pallas kernels  42.6 us (97%)
  between operations  1.29 us (3%)
    pallas_call x1, Pallas kernels, on_device(): pl.pallas_call(kernel, out_shape=(jax.ShapeDtypeStruct((brs, 1, width), f...  42 us

profile of v4, /device:TPU:1, one launch (start us, length us, event | category | flops | bytes accessed | tf_op | source)
XLA Modules:
  0.0 43.9 jit_solution(14677857214977053530)
XLA Ops:
  1.3 42.0 %equilibrate.1 = (f32[32,1,256]{2,1,0:T(1,128)S(1)}, f32[16,1,256]{2,1,0:T(1,128)S(1)}) custom-call(s32[1]{0:T(128)} %bitcast.1.count_ref, s32[1,1,32]{2,1,0:T(1,128)} %brow_hbm.1, s32[1,1,32]{2,1,0:T(1,128)} %bcol_hbm.1, bf16[1,1,32,256,256]{4,3,2,1,0:T(8,128)(2,1)} %tiles_hbm.1), custom_call_target="tpu_custom_call" | custom-call | tf_op jit(solution)/shard_map/equilibrate/pallas_call | solution.py:266
  43.3 0.6 %finish.1 = (f32[32,1,256]{2,1,0:T(1,128)}, f32[16,1,256]{2,1,0:T(1,128)}) custom-call(f32[32,1,256]{2,1,0:T(1,128)S(1)} %get-tuple-element.4.rows, f32[16,1,256]{2,1,0:T(1,128)S(1)} %get-tuple-element.5.cols), custom_call_target="tpu_custom_call" | custom-call | tf_op jit(solution)/shard_map/finish/pallas_call | solution.py:310
